TPU v7x, 32 devices: a whole 2x2x4 slice. The times are simulated.
32 devices in a mesh: ent: 2 (over x), blk: 4 (over y, core), rel: 4 (over z).
Axes of the slice: x: 2, y: 2, z: 4, core: 2. Of those that a mesh axis runs over, the one named last changes fastest.
Arguments:
- factors: bfloat16 [8192, 256], P(('ent', 'blk')), may hold values from -12 to 12
- heads: int32 [8, 4, 1, 8192], P(None, 'rel', None, ('ent', 'blk')), may hold values from 0 to 1023, as said below
- tails: int32 [8, 4, 1, 8192], P(None, 'rel', None, ('ent', 'blk')), may hold values from 0 to 1023, as said below
- values: float32 [8, 4, 1, 8192], P(None, 'rel', None, ('ent', 'blk')), may hold values from 0.3 to 9
Outputs:
- relation_fit: float32 [32, 256, 256], P(('ent', 'blk', 'rel'))
- residual: float32 [32, 256, 256], P(('ent', 'blk', 'rel'))
Inputs may be any that keep to these rules, and one draw needn't show every extreme that they name: In every aligned tile of 128 triple columns (columns 128 t to 128 t + 127 of one relation) all heads lie in one aligned block of 128 positions (128 b to 128 b + 127). In every aligned tile of 128 triple columns all tails lie in one aligned block of 128 positions.
All inputs are finite; a program needn't handle non-finite values.
Results may differ from a plain program's by a relative error of at most 0.0029.
Values sent between devices are 32-bit elements; how exact they have to be, the bound alone decides.
A program may use at most 128 MiB of HBM per device.

v0:
```python
import math
import jax
import jax.numpy as jnp
from jax import lax
from jax.sharding import PartitionSpec as P

ITERS = 8
ridge_weight = 0.01
tile_width = 128


def apply_normal(gram_matrix, stacked):
    left_side = jnp.einsum("ab,kbc->kac", gram_matrix, stacked, precision=lax.Precision.HIGHEST)
    return (
        jnp.einsum("kac,cd->kad", left_side, gram_matrix, precision=lax.Precision.HIGHEST)
        + ridge_weight * stacked
    )


def two_products(residual, image_map):
    return lax.psum(
        (jnp.sum(residual * residual), jnp.sum(residual * image_map)), ("ent", "blk", "rel")
    )


def select_rows(entity_ids, block_table):
    group_size, width = entity_ids.shape
    tile_count = width // tile_width
    block_count = block_table.shape[0]
    tiled_ids = entity_ids.reshape(group_size, tile_count, tile_width)
    block_of = tiled_ids[:, :, 0] // tile_width
    block_pick = (
        block_of[:, :, None] == jnp.arange(block_count, dtype=jnp.int32)[None, None, :]
    ).astype(jnp.bfloat16)
    chosen = jnp.einsum(
        "gtb,bcr->gtcr", block_pick, block_table, preferred_element_type=jnp.float32
    ).astype(jnp.bfloat16)
    inside = tiled_ids % tile_width
    slot_pick = (
        inside[:, :, :, None] == jnp.arange(tile_width, dtype=jnp.int32)[None, None, None, :]
    ).astype(jnp.bfloat16)
    return jnp.einsum("gtoc,gtcr->gtor", slot_pick, chosen, preferred_element_type=jnp.float32)


def body(factors, heads, tails, values):
    shards = lax.axis_size(("ent", "blk"))
    ent_dev = factors.shape[0]
    rank_width = factors.shape[1]
    triple_count = heads.shape[3]
    relation_rows = heads.shape[0] * heads.shape[2]
    norm_scale = 1.0 / math.sqrt(shards * triple_count)
    gram_total = lax.psum(
        jnp.dot(factors.T, factors, preferred_element_type=jnp.float32), ("ent", "blk")
    )
    gram_matrix = gram_total / (ent_dev * shards)
    block_table = factors.reshape(ent_dev // tile_width, tile_width, rank_width)
    head_ids = heads.reshape(relation_rows, triple_count)
    tail_ids = tails.reshape(relation_rows, triple_count)
    weights = values.reshape(relation_rows, triple_count)

    def grouped(operands):
        head_group, tail_group, weight_group = operands
        group_size = head_group.shape[0]
        tile_count = triple_count // tile_width
        head_rows = select_rows(head_group, block_table)
        weighted = (
            weight_group.reshape(group_size, tile_count, tile_width)[:, :, :, None] * head_rows
        ).astype(jnp.bfloat16)
        tail_rows = select_rows(tail_group, block_table).astype(jnp.bfloat16)
        product = jnp.einsum(
            "gtci,gtcj->gij", weighted, tail_rows, preferred_element_type=jnp.float32
        )
        return product * norm_scale

    own_rows = relation_rows // shards
    group_size = math.gcd(own_rows * lax.axis_size(("ent", "blk")), 4)
    group_total = own_rows * lax.axis_size(("ent", "blk")) // group_size
    shaped = (
        head_ids.reshape(group_total, group_size, triple_count),
        tail_ids.reshape(group_total, group_size, triple_count),
        weights.reshape(group_total, group_size, triple_count),
    )
    results = lax.map(grouped, shaped)
    target = lax.psum_scatter(
        results.reshape(own_rows * lax.axis_size(("ent", "blk")), rank_width, rank_width),
        ("ent", "blk"),
        scatter_dimension=0,
        tiled=True,
    )
    fitted = jnp.zeros_like(target)
    residual = target
    image_map = apply_normal(gram_matrix, residual)
    norm_now, product = two_products(residual, image_map)
    step_size = norm_now / product
    direction = residual
    along = image_map
    for step_index in range(ITERS):
        fitted = fitted + step_size * direction
        residual = residual - step_size * along
        if step_index + 1 < ITERS:
            image_map = apply_normal(gram_matrix, residual)
            norm_next, product = two_products(residual, image_map)
            ratio_next = norm_next / norm_now
            step_size = norm_next / (product - ratio_next * norm_next / step_size)
            direction = residual + ratio_next * direction
            along = image_map + ratio_next * along
            norm_now = norm_next
    return (fitted, residual)


def solution(mesh):
    placed = (
        P(("ent", "blk"), None),
        P(None, "rel", None, ("ent", "blk")),
        P(None, "rel", None, ("ent", "blk")),
        P(None, "rel", None, ("ent", "blk")),
    )
    return jax.shard_map(
        body,
        mesh=mesh,
        in_specs=placed,
        out_specs=(P(("ent", "blk", "rel"), None, None), P(("ent", "blk", "rel"), None, None)),
        check_vma=False,
    )
```

profile of v0, /device:TPU:0, one launch (start us, length us, event | category | flops | bytes accessed | tf_op | source)
XLA Modules:
  0.0 491.8 jit_solution(14854573454437355438)
XLA Ops:
  7.2 0.0 copy-start.1
  7.2 0.0 copy-start.3
  7.2 0.0 all-reduce.10.cloned.1.call-start
  7.2 2.3 fusion.80
  9.5 0.0 all-reduce.10.cloned.1.call-update
  9.5 0.0 reduce-scatter.2.cloned.1.call-start
  9.6 0.8 reduce.2
  10.5 0.8 reduce.3
  11.3 0.0 copy-done.1
  11.3 0.3 copy.14
  11.6 0.0 copy-done.3
  11.6 0.1 reduce.4
  11.7 17.5 %while.13 = (s32[]{:T(128)}, f32[2,4,256,256]{3,2,1,0:T(8,128)}, f32[2,4,1024]{2,1,0:T(4,128)S(1)}, s32[2,4,1024]{2,1,0:T(4,128)S(1)}, bf16[8,128,256]{2,0,1:T(8...) while((s32[]{:T(128)}, f32[2,4,256,256]{3,2,1,0:T(8,128)}, f32[2,4,1024]{2,1,0:T(4,128)S(1)}, ...), condition=%wide.region_1.2_spmd, body=%wide.region_0.0_spmd.sunk | while | flops 1113941504 | bytes 14992225 | solution.py:83
  11.8 0.2 fusion.111
  11.9 0.7 convolution_convert_fusion.4
  12.7 2.7 multiply_convert_fusion.2
  15.5 0.2 fusion.112
  15.6 0.7 convolution_convert_fusion.5
  16.4 4.1 fusion.113
  20.5 0.2 fusion.111
  20.7 0.7 convolution_convert_fusion.4
  21.5 2.7 multiply_convert_fusion.2
  24.2 0.2 fusion.112
  24.4 0.7 convolution_convert_fusion.5
  25.1 4.1 fusion.113
  29.3 0.0 reduce-scatter.2.cloned.1.call-update
  29.3 39.0 %all-reduce.10.cloned.1.call-done = f32[256,256]{1,0:T(8,128)} async-done(((f32[256,256]{1,0:T(8,128)}), f32[256,256]{1,0:T(8,128)}) %all-reduce.10.cloned.1.call-update) | async-done | bytes 262160 | tf_op jit(solution)/shard_map/psum | solution.py:52
  68.3 43.8 %reduce-scatter.2.cloned.1.call-done = f32[1,256,256]{2,1,0:T(8,128)} async-done(((f32[8,256,256]{2,1,0:T(8,128)}), f32[1,256,256]{2,1,0:T(8,128)}) %reduce-scatter.2.cloned.1.call-update) | async-done | bytes 262160 | tf_op jit(solution)/shard_map/reduce_scatter | solution.py:84
  112.1 1.6 convolution_bitcast_fusion.15
  113.7 2.2 multiply_reduce_fusion.14
  116.0 39.5 %all-reduce.7 = (f32[]{:T(128)}, f32[]{:T(128)}) all-reduce(f32[]{:T(128)} %get-tuple-element.128, f32[]{:T(128)} %get-tuple-element.127), channel_id=1, replica_groups=mesh['ent'=2,'blk'=4,'rel'=4] {'ent','blk','rel'}, use_global_device_ids=true, to_apply=%region_4.5 | all-reduce | flops 2 | bytes 16 | tf_op jit(solution)/shard_map/psum | solution.py:21
  156.8 1.0 multiply_subtract_fusion.7
  157.8 0.0 copy-done
  157.8 0.6 convolution_bitcast_fusion.13
  158.4 1.3 multiply_reduce_fusion.12
  159.7 41.4 %all-reduce.6 = (f32[]{:T(128)}, f32[]{:T(128)}) all-reduce(f32[]{:T(128)} %get-tuple-element.126, f32[]{:T(128)} %get-tuple-element.125), channel_id=1, replica_groups=mesh['ent'=2,'blk'=4,'rel'=4] {'ent','blk','rel'}, use_global_device_ids=true, to_apply=%region_9.10 | all-reduce | flops 2 | bytes 16 | tf_op jit(solution)/shard_map/psum | solution.py:21
  205.5 0.1 multiply_subtract_fusion.6
  205.5 0.6 convolution_bitcast_fusion.11
  206.1 1.2 multiply_reduce_fusion.10
  207.3 39.6 %all-reduce.5 = (f32[]{:T(128)}, f32[]{:T(128)}) all-reduce(f32[]{:T(128)} %get-tuple-element.124, f32[]{:T(128)} %get-tuple-element.123), channel_id=1, replica_groups=mesh['ent'=2,'blk'=4,'rel'=4] {'ent','blk','rel'}, use_global_device_ids=true, to_apply=%region_13.14 | all-reduce | flops 2 | bytes 16 | tf_op jit(solution)/shard_map/psum | solution.py:21
  250.7 0.1 multiply_subtract_fusion.5
  250.7 0.6 convolution_bitcast_fusion.9
  251.3 1.3 multiply_reduce_fusion.8
  252.6 41.5 %all-reduce.4 = (f32[]{:T(128)}, f32[]{:T(128)}) all-reduce(f32[]{:T(128)} %get-tuple-element.122, f32[]{:T(128)} %get-tuple-element.121), channel_id=1, replica_groups=mesh['ent'=2,'blk'=4,'rel'=4] {'ent','blk','rel'}, use_global_device_ids=true, to_apply=%region_17.18 | all-reduce | flops 2 | bytes 16 | tf_op jit(solution)/shard_map/psum | solution.py:21
  298.1 0.1 multiply_subtract_fusion.4
  298.1 0.6 convolution_bitcast_fusion.7
  298.7 1.2 multiply_reduce_fusion.6
  299.9 39.6 %all-reduce.3 = (f32[]{:T(128)}, f32[]{:T(128)}) all-reduce(f32[]{:T(128)} %get-tuple-element.120, f32[]{:T(128)} %get-tuple-element.119), channel_id=1, replica_groups=mesh['ent'=2,'blk'=4,'rel'=4] {'ent','blk','rel'}, use_global_device_ids=true, to_apply=%region_21.22 | all-reduce | flops 2 | bytes 16 | tf_op jit(solution)/shard_map/psum | solution.py:21
  343.4 0.1 multiply_subtract_fusion.3
  343.5 0.6 convolution_bitcast_fusion.5
  344.1 1.3 multiply_reduce_fusion.4
  345.4 41.3 %all-reduce.2 = (f32[]{:T(128)}, f32[]{:T(128)}) all-reduce(f32[]{:T(128)} %get-tuple-element.118, f32[]{:T(128)} %get-tuple-element.117), channel_id=1, replica_groups=mesh['ent'=2,'blk'=4,'rel'=4] {'ent','blk','rel'}, use_global_device_ids=true, to_apply=%region_25.26 | all-reduce | flops 2 | bytes 16 | tf_op jit(solution)/shard_map/psum | solution.py:21
  390.7 0.1 multiply_subtract_fusion.2
  390.7 0.6 convolution_bitcast_fusion.3
  391.3 1.2 multiply_reduce_fusion.2
  392.5 39.5 %all-reduce.1 = (f32[]{:T(128)}, f32[]{:T(128)}) all-reduce(f32[]{:T(128)} %get-tuple-element.116, f32[]{:T(128)} %get-tuple-element.115), channel_id=1, replica_groups=mesh['ent'=2,'blk'=4,'rel'=4] {'ent','blk','rel'}, use_global_device_ids=true, to_apply=%region_29.30 | all-reduce | flops 2 | bytes 16 | tf_op jit(solution)/shard_map/psum | solution.py:21
  436.0 0.0 copy-start.2
  436.0 0.1 multiply_subtract_fusion.1
  436.1 0.6 convolution_bitcast_fusion.1
  436.7 1.3 multiply_reduce_fusion
  437.9 41.3 %all-reduce = (f32[]{:T(128)}, f32[]{:T(128)}) all-reduce(f32[]{:T(128)} %get-tuple-element.114, f32[]{:T(128)} %get-tuple-element.113), channel_id=1, replica_groups=mesh['ent'=2,'blk'=4,'rel'=4] {'ent','blk','rel'}, use_global_device_ids=true, to_apply=%region_33.34 | all-reduce | flops 2 | bytes 16 | tf_op jit(solution)/shard_map/psum | solution.py:21
  483.2 0.8 multiply_subtract_fusion
  484.0 0.0 copy-done.2
  484.0 1.0 multiply_add_fusion
  (19 shorter events, 0.1 us)
Async XLA Ops:
  7.2 4.2 copy-start.1
  7.2 4.5 copy-start.3
  7.2 61.1 %all-reduce.10.cloned.1.call-start = ((), (), s32[]{:S(2)}) async-start(), calls=%async_computation.2 | async-start | bytes 524288 | tf_op jit(solution)/shard_map/psum | solution.py:52
  9.5 102.6 %reduce-scatter.2.cloned.1.call-start = ((), (), s32[]{:S(2)}) async-start(), calls=%async_computation.1 | async-start | bytes 2359296 | tf_op jit(solution)/shard_map/reduce_scatter | solution.py:84
  68.3 89.5 %copy-start = (f32[256,256]{1,0:T(8,128)S(1)}, f32[256,256]{1,0:T(8,128)}, u32[]{:S(2)}) copy-start(f32[256,256]{1,0:T(8,128)} %all-reduce.10.cloned.1.call-done) | copy-start | bytes 786436
  436.0 48.0 %copy-start.2 = (f32[1,256,256]{2,1,0:T(8,128)S(1)}, f32[1,256,256]{2,1,0:T(8,128)}, u32[]{:S(2)}) copy-start(f32[1,256,256]{2,1,0:T(8,128)} %reduce-scatter.2.cloned.1.call-done) | copy-start | bytes 786436
Sparse Core Ops, SparseCore 0:
  11.6 56.6 all-reduce.9
  71.6 40.4 reduce-scatter.1
where the time goes:
time: 494 us; the launch traced here: 492 us
  blocking collectives  324 us (66%)
  waiting for transfers between devices  82.8 us (17%)
  between operations  43.5 us (9%)
  matrix products  35.6 us (7%)
  other arithmetic  5.49 us (1%)
    psum x8, blocking collectives, two_products(): lax.psum((jnp.sum(residual * residual), jnp.sum(residual * image_map)), (...  324 us
    reduce_scatter x1, waiting for transfers between devices, body(): lax.psum_scatter(results.reshape(own_rows * lax.axis_size(('ent', 'blk'))...  43.8 us
    psum x1, waiting for transfers between devices, body(): lax.psum(jnp.dot(factors.T, factors, preferred_element_type=jnp.float32),...  39 us
    dot_general x8, matrix products, apply_normal(): jnp.einsum('kac,cd->kad', left_side, gram_matrix, precision=lax.Precision...  10.9 us
  transfers between devices with their start and end apart: 2, of which 2 were waited for; matrix products, arithmetic and copies ran while one was open for 4% of the time, Pallas kernels for 0%

commit v1 on v0

--- a/solution.py
+++ b/solution.py
@@ -49,8 +49,11 @@
     triple_count = heads.shape[3]
     relation_rows = heads.shape[0] * heads.shape[2]
     norm_scale = 1.0 / math.sqrt(shards * triple_count)
-    gram_total = lax.psum(
-        jnp.dot(factors.T, factors, preferred_element_type=jnp.float32), ("ent", "blk")
+    gram_total = jnp.sum(
+        lax.all_gather(
+            jnp.dot(factors.T, factors, preferred_element_type=jnp.float32), ("ent", "blk")
+        ),
+        axis=0,
     )
     gram_matrix = gram_total / (ent_dev * shards)
     block_table = factors.reshape(ent_dev // tile_width, tile_width, rank_width)

time: 494 us -> 466 us (0.943)
  waiting for transfers between devices: 82.8 us -> 54.4 us
    psum x1 -> x0, waiting for transfers between devices: 39 us -> none  [body(): lax.psum(jnp.dot(factors.T, factors, preferred_element_type=jnp.float32),...]
    all_gather x0 -> x1, waiting for transfers between devices: none -> 11.7 us  [body(): lax.all_gather(jnp.dot(factors.T, factors, preferred_element_type=jnp.flo...]
  transfers between devices with their start and end apart: 2 -> 2, of which waited for: 2 -> 2; matrix products, arithmetic and copies ran while one was open for 4% -> 5% of each run, Pallas kernels for 0% -> 0%
where the time goes in v1:
time: 466 us; the launch traced here: 464 us
  blocking collectives  324 us (70%)
  waiting for transfers between devices  54.4 us (12%)
  between operations  42.9 us (9%)
  matrix products  35.6 us (8%)
  other arithmetic  7.25 us (2%)
    psum x8, blocking collectives, two_products(): lax.psum((jnp.sum(residual * residual), jnp.sum(residual * image_map)), (...  324 us
    reduce_scatter x1, waiting for transfers between devices, body(): lax.psum_scatter(results.reshape(own_rows * lax.axis_size(('ent', 'blk'))...  42.7 us
    all_gather x1, waiting for transfers between devices, body(): lax.all_gather(jnp.dot(factors.T, factors, preferred_element_type=jnp.flo...  11.7 us
    dot_general x8, matrix products, apply_normal(): jnp.einsum('kac,cd->kad', left_side, gram_matrix, precision=lax.Precision...  10.9 us
  transfers between devices with their start and end apart: 2, of which 2 were waited for; matrix products, arithmetic and copies ran while one was open for 5% of the time, Pallas kernels for 0%

profile of v1, /device:TPU:0, one launch (start us, length us, event | category | flops | bytes accessed | tf_op | source)
XLA Modules:
  0.0 464.3 jit_solution(4138317408375631745)
XLA Ops:
  7.2 0.0 copy-start
  7.2 0.0 copy-start.2
  7.2 0.0 all-gather.3.cloned.1.call-start
  7.2 2.3 fusion.80
  9.5 0.0 all-gather.3.cloned.1.call-update
  9.5 0.0 reduce-scatter.2.cloned.1.call-start
  9.6 0.8 reduce.2
  10.5 0.8 reduce.3
  11.3 0.0 copy-done
  11.3 0.3 copy.14
  11.6 0.0 copy-done.2
  11.6 0.1 reduce.4
  11.7 17.5 %while.13 = (s32[]{:T(128)}, f32[2,4,256,256]{3,2,1,0:T(8,128)}, f32[2,4,1024]{2,1,0:T(4,128)S(1)}, s32[2,4,1024]{2,1,0:T(4,128)S(1)}, bf16[8,128,256]{2,0,1:T(8...) while((s32[]{:T(128)}, f32[2,4,256,256]{3,2,1,0:T(8,128)}, f32[2,4,1024]{2,1,0:T(4,128)S(1)}, ...), condition=%wide.region_1.2_spmd, body=%wide.region_0.0_spmd.sunk | while | flops 1113941504 | bytes 14992225 | solution.py:86
  11.8 0.2 fusion.111
  11.9 0.7 convolution_convert_fusion.4
  12.7 2.7 multiply_convert_fusion.2
  15.5 0.2 fusion.112
  15.6 0.7 convolution_convert_fusion.5
  16.4 4.1 fusion.113
  20.5 0.2 fusion.111
  20.7 0.7 convolution_convert_fusion.4
  21.5 2.7 multiply_convert_fusion.2
  24.2 0.2 fusion.112
  24.4 0.7 convolution_convert_fusion.5
  25.1 4.1 fusion.113
  29.3 0.0 reduce-scatter.2.cloned.1.call-update
  29.3 11.7 %all-gather.3.cloned.1.call-done = f32[2048,256]{1,0:T(8,128)} async-done(((f32[256,256]{1,0:T(8,128)}), f32[2048,256]{1,0:T(8,128)}) %all-gather.3.cloned.1.call-update) | async-done | bytes 2097168 | tf_op jit(solution)/shard_map/all_gather | solution.py:53
  41.0 1.8 reduce_sum.154
  42.8 42.7 %reduce-scatter.2.cloned.1.call-done = f32[1,256,256]{2,1,0:T(8,128)} async-done(((f32[8,256,256]{2,1,0:T(8,128)}), f32[1,256,256]{2,1,0:T(8,128)}) %reduce-scatter.2.cloned.1.call-update) | async-done | bytes 262160 | tf_op jit(solution)/shard_map/reduce_scatter | solution.py:87
  85.4 1.5 convolution_bitcast_fusion.15
  87.0 2.2 multiply_reduce_fusion.14
  89.1 39.5 %all-reduce.7 = (f32[]{:T(128)}, f32[]{:T(128)}) all-reduce(f32[]{:T(128)} %get-tuple-element.128, f32[]{:T(128)} %get-tuple-element.127), channel_id=1, replica_groups=mesh['ent'=2,'blk'=4,'rel'=4] {'ent','blk','rel'}, use_global_device_ids=true, to_apply=%region_4.5 | all-reduce | flops 2 | bytes 16 | tf_op jit(solution)/shard_map/psum | solution.py:21
  130.0 1.0 multiply_subtract_fusion.7
  131.0 0.6 convolution_bitcast_fusion.13
  131.6 1.3 multiply_reduce_fusion.12
  132.8 41.4 %all-reduce.6 = (f32[]{:T(128)}, f32[]{:T(128)}) all-reduce(f32[]{:T(128)} %get-tuple-element.126, f32[]{:T(128)} %get-tuple-element.125), channel_id=1, replica_groups=mesh['ent'=2,'blk'=4,'rel'=4] {'ent','blk','rel'}, use_global_device_ids=true, to_apply=%region_9.10 | all-reduce | flops 2 | bytes 16 | tf_op jit(solution)/shard_map/psum | solution.py:21
  178.8 0.1 multiply_subtract_fusion.6
  178.9 0.6 convolution_bitcast_fusion.11
  179.5 1.2 multiply_reduce_fusion.10
  180.7 39.5 %all-reduce.5 = (f32[]{:T(128)}, f32[]{:T(128)}) all-reduce(f32[]{:T(128)} %get-tuple-element.124, f32[]{:T(128)} %get-tuple-element.123), channel_id=1, replica_groups=mesh['ent'=2,'blk'=4,'rel'=4] {'ent','blk','rel'}, use_global_device_ids=true, to_apply=%region_13.14 | all-reduce | flops 2 | bytes 16 | tf_op jit(solution)/shard_map/psum | solution.py:21
  224.1 0.1 multiply_subtract_fusion.5
  224.2 0.6 convolution_bitcast_fusion.9
  224.8 1.3 multiply_reduce_fusion.8
  226.1 41.5 %all-reduce.4 = (f32[]{:T(128)}, f32[]{:T(128)}) all-reduce(f32[]{:T(128)} %get-tuple-element.122, f32[]{:T(128)} %get-tuple-element.121), channel_id=1, replica_groups=mesh['ent'=2,'blk'=4,'rel'=4] {'ent','blk','rel'}, use_global_device_ids=true, to_apply=%region_17.18 | all-reduce | flops 2 | bytes 16 | tf_op jit(solution)/shard_map/psum | solution.py:21
  271.3 0.1 multiply_subtract_fusion.4
  271.4 0.6 convolution_bitcast_fusion.7
  272.0 1.2 multiply_reduce_fusion.6
  273.2 39.5 %all-reduce.3 = (f32[]{:T(128)}, f32[]{:T(128)}) all-reduce(f32[]{:T(128)} %get-tuple-element.120, f32[]{:T(128)} %get-tuple-element.119), channel_id=1, replica_groups=mesh['ent'=2,'blk'=4,'rel'=4] {'ent','blk','rel'}, use_global_device_ids=true, to_apply=%region_21.22 | all-reduce | flops 2 | bytes 16 | tf_op jit(solution)/shard_map/psum | solution.py:21
  316.5 0.1 multiply_subtract_fusion.3
  316.6 0.6 convolution_bitcast_fusion.5
  317.2 1.3 multiply_reduce_fusion.4
  318.5 41.3 %all-reduce.2 = (f32[]{:T(128)}, f32[]{:T(128)}) all-reduce(f32[]{:T(128)} %get-tuple-element.118, f32[]{:T(128)} %get-tuple-element.117), channel_id=1, replica_groups=mesh['ent'=2,'blk'=4,'rel'=4] {'ent','blk','rel'}, use_global_device_ids=true, to_apply=%region_25.26 | all-reduce | flops 2 | bytes 16 | tf_op jit(solution)/shard_map/psum | solution.py:21
  363.6 0.1 multiply_subtract_fusion.2
  363.6 0.6 convolution_bitcast_fusion.3
  364.2 1.2 multiply_reduce_fusion.2
  365.4 39.5 %all-reduce.1 = (f32[]{:T(128)}, f32[]{:T(128)}) all-reduce(f32[]{:T(128)} %get-tuple-element.116, f32[]{:T(128)} %get-tuple-element.115), channel_id=1, replica_groups=mesh['ent'=2,'blk'=4,'rel'=4] {'ent','blk','rel'}, use_global_device_ids=true, to_apply=%region_29.30 | all-reduce | flops 2 | bytes 16 | tf_op jit(solution)/shard_map/psum | solution.py:21
  408.7 0.0 copy-start.1
  408.7 0.1 multiply_subtract_fusion.1
  408.8 0.6 convolution_bitcast_fusion.1
  409.4 1.3 multiply_reduce_fusion
  410.7 41.3 %all-reduce = (f32[]{:T(128)}, f32[]{:T(128)}) all-reduce(f32[]{:T(128)} %get-tuple-element.114, f32[]{:T(128)} %get-tuple-element.113), channel_id=1, replica_groups=mesh['ent'=2,'blk'=4,'rel'=4] {'ent','blk','rel'}, use_global_device_ids=true, to_apply=%region_33.34 | all-reduce | flops 2 | bytes 16 | tf_op jit(solution)/shard_map/psum | solution.py:21
  455.7 0.8 multiply_subtract_fusion
  456.5 0.0 copy-done.1
  456.5 1.0 multiply_add_fusion
  (18 shorter events, 0.1 us)
Async XLA Ops:
  7.2 4.2 copy-start
  7.2 4.5 copy-start.2
  7.2 33.8 %all-gather.3.cloned.1.call-start = ((), (), s32[]{:S(2)}) async-start(), calls=%async_computation.2 | async-start | bytes 2359296 | tf_op jit(solution)/shard_map/all_gather | solution.py:53
  9.5 75.9 %reduce-scatter.2.cloned.1.call-start = ((), (), s32[]{:S(2)}) async-start(), calls=%async_computation.1 | async-start | bytes 2359296 | tf_op jit(solution)/shard_map/reduce_scatter | solution.py:87
  408.7 47.8 %copy-start.1 = (f32[1,256,256]{2,1,0:T(8,128)S(1)}, f32[1,256,256]{2,1,0:T(8,128)}, u32[]{:S(2)}) copy-start(f32[1,256,256]{2,1,0:T(8,128)} %reduce-scatter.2.cloned.1.call-done) | copy-start | bytes 786436
Sparse Core Ops, SparseCore 0:
  10.5 30.4 all-gather.2
  44.3 41.0 reduce-scatter.1
